TPU v7x, 32 devices: a whole 2x2x4 slice. The times are simulated.
32 devices in a mesh: lat: 4 (over y, x), lon: 8 (over z, core).
Axes of the slice: x: 2, y: 2, z: 4, core: 2. Of those that a mesh axis runs over, the one named last changes fastest.
Arguments:
- right_side: float32 [8, 768, 1024], P(None, 'lat', 'lon'), may hold values from -16 to 16
- center: float32 [768, 1024], P('lat', 'lon'), may hold values from 3.7 to 5.5
- couplings: float32 [4, 768, 1024], P(None, 'lat', 'lon'), may hold values from 0.15 to 0.45
- land_sea: int32 [768, 1024], P('lat', 'lon'), may hold values 0 or 1
- fold_partner: int32 [1024], replicated, may hold values from 0 to 1023, as said below
Outputs:
- solution: float32 [8, 768, 1024], P(None, 'lat', 'lon')
- residual: float32 [8, 768, 1024], P(None, 'lat', 'lon')
Inputs may be any that keep to these rules, and one draw needn't show every extreme that they name: fold_partner[i] = (s - i) mod 1024 for one integer s, so fold_partner[fold_partner[i]] = i.
All inputs are finite; a program needn't handle non-finite values. No bound on the sum of `land_sea` on one device may be relied on, other than what follows from the above.
Results may differ from a plain program's by a relative error of at most 0.0003.
Values sent between devices are 32-bit elements; how exact they have to be, the bound alone decides.
A program may use at most 64 MiB of HBM per device.

v0:
```python
import jax
import jax.numpy as jnp
from jax import lax
from jax.sharding import PartitionSpec as P

ITERS = 3


def extended(cells, sides, width, closed):
    for axis, dim in sides:
        count = lax.axis_size(axis)
        ends = count if closed else count - 1
        head = lax.slice_in_dim(cells, 0, width, axis=dim)
        tail = lax.slice_in_dim(cells, cells.shape[dim] - width, cells.shape[dim], axis=dim)
        cells = jnp.concatenate(
            [
                lax.ppermute(tail, axis, [(i, (i + 1) % count) for i in range(ends)]),
                cells,
                lax.ppermute(head, axis, [((i + 1) % count, i) for i in range(ends)]),
            ],
            axis=dim,
        )
    return cells


def body(right_side, center, couplings, land_sea, fold_partner):
    row_count, col_count = center.shape
    lat_last = lax.axis_index("lat") == lax.axis_size("lat") - 1
    lat_first = lax.axis_index("lat") == 0
    first_col = lax.axis_index("lon") * col_count
    partner_local = lax.dynamic_slice_in_dim(fold_partner, first_col, col_count, 0)
    ocean_mask = land_sea.astype(jnp.float32)
    north_top = couplings[1, -1, :]
    whole_north = lax.all_gather(north_top, "lon", axis=0, tiled=True)
    fold_coeff = 0.5 * (north_top + jnp.take(whole_north, partner_local, axis=0))
    row_index = lax.broadcasted_iota(jnp.int32, (row_count, col_count), 0)
    top_rows = jnp.logical_and(lat_last, row_index == row_count - 1)
    east_coeff = couplings[0]
    north_coeff = jnp.where(top_rows, fold_coeff[None, :], couplings[1])
    northeast = jnp.where(top_rows, 0.0, couplings[2])
    northwest = jnp.where(top_rows, 0.0, couplings[3])
    stacked = jnp.stack([east_coeff, north_coeff, northeast, northwest])
    coeff_padded = extended(stacked, (("lat", 1), ("lon", 2)), 1, True)
    ghost_rows = lax.broadcasted_iota(jnp.int32, (1, row_count + 2, col_count + 2), 1)
    coeff_padded = jnp.where(jnp.logical_and(lat_first, ghost_rows == 0), 0.0, coeff_padded)
    west_coeff = coeff_padded[0, 1:-1, :-2]
    south_coeff = coeff_padded[1, :-2, 1:-1]
    southwest = coeff_padded[2, :-2, :-2]
    southeast = coeff_padded[3, :-2, 2:]

    def operate(vector):
        top_row = vector[:, -1, :]
        whole_top = lax.all_gather(top_row, "lon", axis=1, tiled=True)
        fold_ghost = jnp.take(whole_top, partner_local, axis=1)
        lon_padded = extended(vector, (("lon", 2),), 1, True)
        padded = extended(lon_padded, (("lat", 1),), 1, False)
        north_row = jnp.where(lat_last, fold_ghost, padded[:, -1, 1:-1])
        padded = padded.at[:, -1, 1:-1].set(north_row)
        upper = padded[:, 2:, 1:-1]
        lower = padded[:, :-2, 1:-1]
        beside = east_coeff * padded[:, 1:-1, 2:] + west_coeff * padded[:, 1:-1, :-2]
        beside = beside + north_coeff * upper + south_coeff * lower
        beside = beside + northeast * padded[:, 2:, 2:] + southwest * padded[:, :-2, :-2]
        beside = beside + northwest * padded[:, 2:, :-2] + southeast * padded[:, :-2, 2:]
        return ocean_mask * (center * vector - beside)

    def paired_sums(residual, scaled, image):
        return lax.psum(
            (jnp.sum(residual * scaled, axis=(1, 2)), jnp.sum(scaled * image, axis=(1, 2))),
            ("lat", "lon"),
        )

    residual = right_side * ocean_mask
    solution = jnp.zeros_like(residual)
    scaled = residual / center
    image = operate(scaled)
    gamma_now, curve = paired_sums(residual, scaled, image)
    step_size = gamma_now / curve
    direction = scaled
    along_dir = image
    for iteration in range(ITERS):
        solution = solution + step_size[:, None, None] * direction
        residual = residual - step_size[:, None, None] * along_dir
        if iteration + 1 < ITERS:
            scaled = residual / center
            image = operate(scaled)
            gamma_next, curve = paired_sums(residual, scaled, image)
            beta_ratio = gamma_next / gamma_now
            step_size = gamma_next / (curve - beta_ratio * gamma_next / step_size)
            direction = scaled + beta_ratio[:, None, None] * direction
            along_dir = image + beta_ratio[:, None, None] * along_dir
            gamma_now = gamma_next
    return (solution, residual)


def solution(mesh):
    return jax.shard_map(
        body,
        mesh=mesh,
        in_specs=(
            P(None, "lat", "lon"),
            P("lat", "lon"),
            P(None, "lat", "lon"),
            P("lat", "lon"),
            P(),
        ),
        out_specs=(P(None, "lat", "lon"), P(None, "lat", "lon")),
        check_vma=False,
    )
```

profile of v0, /device:TPU:0, one launch (start us, length us, event | category | flops | bytes accessed | tf_op | source)
XLA Modules:
  0.0 254.5 jit_solution(16460176406055515500)
XLA Ops:
  0.7 0.8 slice.247
  1.4 13.4 %all-gather.1 = f32[1,1,1024]{2,1,0:T(1,128)S(1)} all-gather(f32[1,1,128]{2,1,0:T(1,128)S(1)} %slice.247), channel_id=3, replica_groups=mesh['lat'=4,'lon'=8] {'lon'}, dimensions={2}, use_global_device_ids=true | all-gather | bytes 4608 | tf_op jit(solution)/shard_map/all_gather | solution.py:34
  14.9 0.8 compare_and_fusion
  15.7 1.0 gather_fusion
  16.6 0.7 fusion.30
  17.3 1.7 slice_select_fusion.2
  19.0 1.5 collective-permute-start.4
  20.6 1.4 collective-permute-start.5
  22.1 1.1 fusion.37
  23.3 1.5 copy.91
  25.7 1.0 fusion.38
  26.7 1.0 collective-permute-start.6
  27.7 2.5 collective-permute-start.7
  30.2 13.8 %all-gather = f32[8,1,1024]{2,1,0:T(1,128)S(1)} all-gather(f32[8,1,128]{2,1,0:T(1,128)S(1)} %slice.304), channel_id=2, replica_groups=mesh['lat'=4,'lon'=8] {'lon'}, dimensions={2}, use_global_device_ids=true | all-gather | bytes 36864 | tf_op jit(solution)/shard_map/all_gather | solution.py:53
  45.4 2.4 maximum_select_fusion
  48.5 2.5 collective-permute-start.2
  51.0 1.3 collective-permute-start.3
  52.3 2.0 slice_bitcast_fusion.3
  54.3 2.7 %collective-permute-done.3 = f32[8,1,130]{2,0,1:T(8,128)S(1)} collective-permute-done((f32[8,1,130]{2,0,1:T(8,128)S(1)}, f32[8,1,130]{2,0,1:T(8,128)S(1)}, u32[]{:S(2)}, u32[]{:S(2)}) %collective-permute-start.3) | collective-permute-done | bytes 4192 | tf_op jit(solution)/shard_map/ppermute | solution.py:19
  57.0 0.7 pad_maximum_fusion.2
  58.2 1.3 scatter.10
  59.6 2.5 multiply_reduce_fusion.4
  62.1 39.8 %all-reduce.2 = (f32[8]{0:T(128)S(1)}, f32[8]{0:T(128)S(1)}) all-reduce(f32[8]{0:T(128)S(1)} %get-tuple-element.50, f32[8]{0:T(128)S(1)} %get-tuple-element.49), channel_id=1, replica_groups=mesh['lat'=4,'lon'=8] {'lat','lon'}, use_global_device_ids=true, to_apply=%region_1.2 | all-reduce | flops 16 | bytes 128 | tf_op jit(solution)/shard_map/psum | solution.py:68
  101.9 2.0 broadcast_divide_fusion.1
  104.9 3.5 %collective-permute-start.9 = (f32[8,192,1]{1,0,2:T(8,128)S(1)}, f32[8,192,1]{1,0,2:T(8,128)S(1)}, u32[]{:S(2)}, u32[]{:S(2)}) collective-permute-start(f32[8,192,1]{1,0,2:T(8,128)S(1)} %copy.100), channel_id=1, source_target_pairs={{1,0},{2,1},{3,2},{4,3},{5,4},{6,5},{7,6},{0,7},{9,8},{10,9},{11,1... | collective-permute-start | bytes 18440 | tf_op jit(solution)/shard_map/ppermute | solution.py:19
  108.4 1.0 collective-permute-done.8
  110.3 1.3 collective-permute-start.11
  111.6 4.8 %collective-permute-start.10 = (f32[8,1,130]{2,0,1:T(8,128)S(1)}, f32[8,1,130]{2,0,1:T(8,128)S(1)}, u32[]{:S(2)}, u32[]{:S(2)}) collective-permute-start(f32[8,1,130]{2,0,1:T(8,128)S(1)} %copy.103), channel_id=1, source_target_pairs={{0,8},{8,16},{16,24},{1,9},{9,17},{17,25},{2,10},{10,18},{18,26},{... | collective-permute-start | bytes 12488 | tf_op jit(solution)/shard_map/ppermute | solution.py:17
  116.4 9.9 %all-gather.2 = f32[8,1,1024]{2,1,0:T(1,128)S(1)} all-gather(f32[8,1,128]{2,1,0:T(1,128)S(1)} %slice.322), channel_id=4, replica_groups=mesh['lat'=4,'lon'=8] {'lon'}, dimensions={2}, use_global_device_ids=true | all-gather | bytes 36864 | tf_op jit(solution)/shard_map/all_gather | solution.py:53
  126.3 1.0 copy.121
  127.3 1.7 gather_fusion.2
  129.1 2.1 pad_maximum_fusion
  131.3 1.3 scatter.11
  132.7 3.4 %multiply_reduce_fusion.2 = (f32[8]{0:T(128)S(1)}, f32[8]{0:T(128)S(1)}, f32[8,192,128]{2,1,0:T(8,128)}) fusion(f32[8,192,128]{2,1,0:T(8,128)} %get-tuple-element.71, f32[192,128]{1,0:T(8,128)} %param.14, f32[8,194,130]{2,1,0:T(8,128)S(1)} %scatter.11, f32[192,128]{1,0:T(8,128)} %get-tuple-element.82, f32[192,128]{1,0:T(8,128)S(1)} %bitcast.51, ...), kind=kLoop, calls=%fused_computation.65 | loop fusion | flops 4521968 | bytes 8847424 | tf_op jit(solution)/shard_map/reduce_sum | solution.py:69
  136.0 39.6 %all-reduce.1 = (f32[8]{0:T(128)S(1)}, f32[8]{0:T(128)S(1)}) all-reduce(f32[8]{0:T(128)S(1)} %get-tuple-element.54, f32[8]{0:T(128)S(1)} %get-tuple-element.53), channel_id=1, replica_groups=mesh['lat'=4,'lon'=8] {'lat','lon'}, use_global_device_ids=true, to_apply=%region_5.7 | all-reduce | flops 16 | bytes 128 | tf_op jit(solution)/shard_map/psum | solution.py:68
  176.2 2.8 %broadcast_divide_fusion = (f32[8,192,128]{2,1,0:T(8,128)S(1)}, f32[8,192,128]{2,1,0:T(8,128)}) fusion(f32[192,128]{1,0:T(8,128)} %param.14, f32[8,192,128]{2,1,0:T(8,128)} %get-tuple-element.71, f32[8,192,128]{2,1,0:T(8,128)} %get-tuple-element.69, f32[8,192,128]{2,1,0:T(8,128)} %copy-done.1, f32[8]{0:T(128)S(1)} %get-tuple-element.68, ...), kind=kLoop, calls=%fused_computation.72 | loop fusion | flops 983040 | bytes 4030528 | tf_op jit(solution)/shard_map/div | solution.py:85
  180.0 3.5 %collective-permute-start.13 = (f32[8,192,1]{1,0,2:T(8,128)S(1)}, f32[8,192,1]{1,0,2:T(8,128)S(1)}, u32[]{:S(2)}, u32[]{:S(2)}) collective-permute-start(f32[8,192,1]{1,0,2:T(8,128)S(1)} %copy.110), channel_id=1, source_target_pairs={{1,0},{2,1},{3,2},{4,3},{5,4},{6,5},{7,6},{0,7},{9,8},{10,9},{11,1... | collective-permute-start | bytes 18440 | tf_op jit(solution)/shard_map/ppermute | solution.py:19
  183.6 1.0 collective-permute-done.12
  185.4 1.3 collective-permute-start.15
  186.7 4.8 %collective-permute-start.14 = (f32[8,1,130]{2,0,1:T(8,128)S(1)}, f32[8,1,130]{2,0,1:T(8,128)S(1)}, u32[]{:S(2)}, u32[]{:S(2)}) collective-permute-start(f32[8,1,130]{2,0,1:T(8,128)S(1)} %copy.113), channel_id=1, source_target_pairs={{0,8},{8,16},{16,24},{1,9},{9,17},{17,25},{2,10},{10,18},{18,26},{... | collective-permute-start | bytes 12488 | tf_op jit(solution)/shard_map/ppermute | solution.py:17
  191.5 9.9 %all-gather.3 = f32[8,1,1024]{2,1,0:T(1,128)S(1)} all-gather(f32[8,1,128]{2,1,0:T(1,128)S(1)} %slice.334), channel_id=5, replica_groups=mesh['lat'=4,'lon'=8] {'lon'}, dimensions={2}, use_global_device_ids=true | all-gather | bytes 36864 | tf_op jit(solution)/shard_map/all_gather | solution.py:53
  201.5 1.0 copy.122
  202.5 1.7 gather_fusion.3
  204.3 2.1 pad_maximum_fusion.1
  206.5 1.3 scatter.14
  207.9 3.5 %multiply_reduce_fusion = (f32[8]{0:T(128)S(1)}, f32[8]{0:T(128)S(1)}, f32[8,192,128]{2,1,0:T(8,128)}) fusion(f32[8,192,128]{2,1,0:T(8,128)} %get-tuple-element.65, f32[192,128]{1,0:T(8,128)} %param.14, f32[8,194,130]{2,1,0:T(8,128)S(1)} %scatter.14, f32[192,128]{1,0:T(8,128)} %get-tuple-element.82, f32[192,128]{1,0:T(8,128)S(1)} %bitcast.52, ...), kind=kLoop, calls=%fused_computation.61 | loop fusion | flops 4521968 | bytes 8847424 | tf_op jit(solution)/shard_map/reduce_sum | solution.py:69
  211.3 39.4 %all-reduce = (f32[8]{0:T(128)S(1)}, f32[8]{0:T(128)S(1)}) all-reduce(f32[8]{0:T(128)S(1)} %get-tuple-element.52, f32[8]{0:T(128)S(1)} %get-tuple-element.51), channel_id=1, replica_groups=mesh['lat'=4,'lon'=8] {'lat','lon'}, use_global_device_ids=true, to_apply=%region_9.11 | all-reduce | flops 16 | bytes 128 | tf_op jit(solution)/shard_map/psum | solution.py:68
  250.8 3.7 %multiply_subtract_fusion = (f32[8,192,128]{2,1,0:T(8,128)}, f32[8,192,128]{2,1,0:T(8,128)}) fusion(f32[8,192,128]{2,1,0:T(8,128)} %get-tuple-element.65, f32[8,192,128]{2,1,0:T(8,128)} %get-tuple-element.63, f32[8]{0:T(128)S(1)} %get-tuple-element.62, f32[8]{0:T(128)S(1)} %get-tuple-element.61, f32[8,192,128]{2,1,0:T(8,128)} %get-tuple-element.69, ...), kind=kLoop, calls=%fused_computation.59 | loop fusion | flops 3735552 | bytes 6488224 | tf_op jit(solution)/shard_map/sub | solution.py:83
  (106 shorter events, 8.3 us)
Async XLA Ops:
  0.6 21.4 %copy-start.9 = (s32[192,128]{1,0:T(8,128)S(1)}, s32[192,128]{1,0:T(8,128)}, u32[]{:S(2)}) copy-start(s32[192,128]{1,0:T(8,128)} %param.16) | copy-start | bytes 294916
  0.6 21.4 %copy-start.8 = (f32[192,128]{1,0:T(8,128)S(1)}, f32[192,128]{1,0:T(8,128)}, u32[]{:S(2)}) copy-start(f32[192,128]{1,0:T(8,128)} %param.14) | copy-start | bytes 294916
  0.7 21.4 %copy-start = (f32[8,192,128]{2,1,0:T(8,128)S(1)}, f32[8,192,128]{2,1,0:T(8,128)}, u32[]{:S(2)}) copy-start(f32[8,192,128]{2,1,0:T(8,128)} %param.13) | copy-start | bytes 2359300
  19.0 26.3 %copy-start.7 = (f32[1,192,128]{2,1,0:T(8,128)}, f32[1,192,128]{2,1,0:T(8,128)S(1)}, u32[]{:S(2)}) copy-start(f32[1,192,128]{2,1,0:T(8,128)S(1)} %get-tuple-element.97) | copy-start | bytes 294916
  19.0 6.6 %collective-permute-start.4 = (f32[4,1,128]{2,1,0:T(1,128)S(1)}, f32[4,1,128]{2,1,0:T(1,128)S(1)}, u32[]{:S(2)}, u32[]{:S(2)}) collective-permute-start(f32[4,1,128]{2,1,0:T(1,128)S(1)} %get-tuple-element.99), channel_id=1, source_target_pairs={{0,8},{8,16},{16,24},{24,0},{1,9},{9,17},{17,25},{25,1},{2,10},{10... | collective-permute-start | bytes 6152 | tf_op jit(solution)/shard_map/ppermute | solution.py:17
  20.6 5.0 %collective-permute-start.5 = (f32[4,1,128]{2,1,0:T(1,128)S(1)}, f32[4,1,128]{2,1,0:T(1,128)S(1)}, u32[]{:S(2)}, u32[]{:S(2)}) collective-permute-start(f32[4,1,128]{2,1,0:T(1,128)S(1)} %get-tuple-element.100), channel_id=1, source_target_pairs={{8,0},{16,8},{24,16},{0,24},{9,1},{17,9},{25,17},{1,25},{10,2},{18... | collective-permute-start | bytes 6152 | tf_op jit(solution)/shard_map/ppermute | solution.py:19
  24.7 23.4 %collective-permute-start.1 = (f32[8,192,1]{1,0,2:T(8,128)S(1)}, f32[8,192,1]{1,0,2:T(8,128)S(1)}, u32[]{:S(2)}, u32[]{:S(2)}) collective-permute-start(f32[8,192,1]{1,0,2:T(8,128)S(1)} %copy.91), channel_id=1, source_target_pairs={{1,0},{2,1},{3,2},{4,3},{5,4},{6,5},{7,6},{0,7},{9,8},{10,9},{11,1... | collective-permute-start | bytes 18440 | tf_op jit(solution)/shard_map/ppermute | solution.py:19
  25.1 22.7 %collective-permute-start = (f32[8,192,1]{1,0,2:T(8,128)S(1)}, f32[8,192,1]{1,0,2:T(8,128)S(1)}, u32[]{:S(2)}, u32[]{:S(2)}) collective-permute-start(f32[8,192,1]{1,0,2:T(8,128)S(1)} %copy.90), channel_id=1, source_target_pairs={{0,1},{1,2},{2,3},{3,4},{4,5},{5,6},{6,7},{7,0},{8,9},{9,10},{10,1... | collective-permute-start | bytes 18440 | tf_op jit(solution)/shard_map/ppermute | solution.py:17
  26.7 18.7 %collective-permute-start.6 = (f32[4,194,1]{2,1,0:T(8,128)}, f32[4,194,1]{2,1,0:T(8,128)S(1)}, u32[]{:S(2)}, u32[]{:S(2)}) collective-permute-start(f32[4,194,1]{2,1,0:T(8,128)} %get-tuple-element.93), channel_id=1, source_target_pairs={{0,1},{1,2},{2,3},{3,4},{4,5},{5,6},{6,7},{7,0},{8,9},{9,10},{10,1... | collective-permute-start | bytes 9320 | tf_op jit(solution)/shard_map/ppermute | solution.py:17
  27.7 17.6 %collective-permute-start.7 = (f32[4,194,1]{2,1,0:T(8,128)}, f32[4,194,1]{2,1,0:T(8,128)}, u32[]{:S(2)}, u32[]{:S(2)}) collective-permute-start(f32[4,194,1]{2,1,0:T(8,128)} %get-tuple-element.94), channel_id=1, source_target_pairs={{1,0},{2,1},{3,2},{4,3},{5,4},{6,5},{7,6},{0,7},{9,8},{10,9},{11,1... | collective-permute-start | bytes 9320 | tf_op jit(solution)/shard_map/ppermute | solution.py:19
  48.5 5.8 %collective-permute-start.2 = (f32[8,1,130]{2,0,1:T(8,128)S(1)}, f32[8,1,130]{2,0,1:T(8,128)S(1)}, u32[]{:S(2)}, u32[]{:S(2)}) collective-permute-start(f32[8,1,130]{2,0,1:T(8,128)S(1)} %get-tuple-element.79), channel_id=1, source_target_pairs={{0,8},{8,16},{16,24},{1,9},{9,17},{17,25},{2,10},{10,18},{18,26},{... | collective-permute-start | bytes 12488 | tf_op jit(solution)/shard_map/ppermute | solution.py:17
  51.0 5.9 %collective-permute-start.3 = (f32[8,1,130]{2,0,1:T(8,128)S(1)}, f32[8,1,130]{2,0,1:T(8,128)S(1)}, u32[]{:S(2)}, u32[]{:S(2)}) collective-permute-start(f32[8,1,130]{2,0,1:T(8,128)S(1)} %get-tuple-element.80), channel_id=1, source_target_pairs={{8,0},{16,8},{24,16},{9,1},{17,9},{25,17},{10,2},{18,10},{26,18},{... | collective-permute-start | bytes 12488 | tf_op jit(solution)/shard_map/ppermute | solution.py:19
  62.1 41.8 %copy-start.1 = (f32[8,192,128]{2,1,0:T(8,128)}, f32[8,192,128]{2,1,0:T(8,128)S(1)}, u32[]{:S(2)}) copy-start(f32[8,192,128]{2,1,0:T(8,128)S(1)} %get-tuple-element.72) | copy-start | bytes 2359300
  101.9 2.0 copy-start.17
  101.9 2.0 copy-start.19
  101.9 2.0 copy-start.15
  104.5 4.9 %collective-permute-start.8 = (f32[8,192,1]{1,0,2:T(8,128)S(1)}, f32[8,192,1]{1,0,2:T(8,128)S(1)}, u32[]{:S(2)}, u32[]{:S(2)}) collective-permute-start(f32[8,192,1]{1,0,2:T(8,128)S(1)} %copy.99), channel_id=1, source_target_pairs={{0,1},{1,2},{2,3},{3,4},{4,5},{5,6},{6,7},{7,0},{8,9},{9,10},{10,1... | collective-permute-start | bytes 18440 | tf_op jit(solution)/shard_map/ppermute | solution.py:17
  104.9 4.9 %collective-permute-start.9 = (f32[8,192,1]{1,0,2:T(8,128)S(1)}, f32[8,192,1]{1,0,2:T(8,128)S(1)}, u32[]{:S(2)}, u32[]{:S(2)}) collective-permute-start(f32[8,192,1]{1,0,2:T(8,128)S(1)} %copy.100), channel_id=1, source_target_pairs={{1,0},{2,1},{3,2},{4,3},{5,4},{6,5},{7,6},{0,7},{9,8},{10,9},{11,1... | collective-permute-start | bytes 18440 | tf_op jit(solution)/shard_map/ppermute | solution.py:19
  109.7 17.6 %copy-start.4 = (f32[8,192,1]{2,1,0:T(8,128)}, f32[8,192,1]{2,1,0:T(8,128)S(1)}, u32[]{:S(2)}) copy-start(f32[8,192,1]{2,1,0:T(8,128)S(1)} %copy.101) | copy-start | bytes 18436
  110.1 19.0 %copy-start.6 = (f32[8,192,1]{2,1,0:T(8,128)}, f32[8,192,1]{2,1,0:T(8,128)S(1)}, u32[]{:S(2)}) copy-start(f32[8,192,1]{2,1,0:T(8,128)S(1)} %copy.102) | copy-start | bytes 18436
  110.3 18.8 %collective-permute-start.11 = (f32[8,1,130]{2,0,1:T(8,128)S(1)}, f32[8,1,130]{2,0,1:T(8,128)S(1)}, u32[]{:S(2)}, u32[]{:S(2)}) collective-permute-start(f32[8,1,130]{2,0,1:T(8,128)S(1)} %copy.123), channel_id=1, source_target_pairs={{8,0},{16,8},{24,16},{9,1},{17,9},{25,17},{10,2},{18,10},{26,18},{... | collective-permute-start | bytes 12488 | tf_op jit(solution)/shard_map/ppermute | solution.py:19
  111.6 17.5 %collective-permute-start.10 = (f32[8,1,130]{2,0,1:T(8,128)S(1)}, f32[8,1,130]{2,0,1:T(8,128)S(1)}, u32[]{:S(2)}, u32[]{:S(2)}) collective-permute-start(f32[8,1,130]{2,0,1:T(8,128)S(1)} %copy.103), channel_id=1, source_target_pairs={{0,8},{8,16},{16,24},{1,9},{9,17},{17,25},{2,10},{10,18},{18,26},{... | collective-permute-start | bytes 12488 | tf_op jit(solution)/shard_map/ppermute | solution.py:17
  132.6 43.0 %copy-start.18 = (f32[8]{0:T(128)S(1)}, f32[8]{0:T(128)}, u32[]{:S(2)}) copy-start(f32[8]{0:T(128)} %copy-done.17) | copy-start | bytes 100
  132.7 43.0 %copy-start.20 = (f32[8]{0:T(128)S(1)}, f32[8]{0:T(128)}, u32[]{:S(2)}) copy-start(f32[8]{0:T(128)} %copy-done.19) | copy-start | bytes 100
  175.6 3.4 %copy-start.12 = (f32[8]{0:T(128)}, f32[8]{0:T(128)S(1)}, u32[]{:S(2)}) copy-start(f32[8]{0:T(128)S(1)} %get-tuple-element.57) | copy-start | bytes 100
  176.2 2.8 %copy-start.10 = (f32[8]{0:T(128)}, f32[8]{0:T(128)S(1)}, u32[]{:S(2)}) copy-start(f32[8]{0:T(128)S(1)} %get-tuple-element.68) | copy-start | bytes 100
  179.7 4.9 %collective-permute-start.12 = (f32[8,192,1]{1,0,2:T(8,128)S(1)}, f32[8,192,1]{1,0,2:T(8,128)S(1)}, u32[]{:S(2)}, u32[]{:S(2)}) collective-permute-start(f32[8,192,1]{1,0,2:T(8,128)S(1)} %copy.109), channel_id=1, source_target_pairs={{0,1},{1,2},{2,3},{3,4},{4,5},{5,6},{6,7},{7,0},{8,9},{9,10},{10,1... | collective-permute-start | bytes 18440 | tf_op jit(solution)/shard_map/ppermute | solution.py:17
  180.0 4.9 %collective-permute-start.13 = (f32[8,192,1]{1,0,2:T(8,128)S(1)}, f32[8,192,1]{1,0,2:T(8,128)S(1)}, u32[]{:S(2)}, u32[]{:S(2)}) collective-permute-start(f32[8,192,1]{1,0,2:T(8,128)S(1)} %copy.110), channel_id=1, source_target_pairs={{1,0},{2,1},{3,2},{4,3},{5,4},{6,5},{7,6},{0,7},{9,8},{10,9},{11,1... | collective-permute-start | bytes 18440 | tf_op jit(solution)/shard_map/ppermute | solution.py:19
  184.9 17.6 %copy-start.3 = (f32[8,192,1]{2,1,0:T(8,128)}, f32[8,192,1]{2,1,0:T(8,128)S(1)}, u32[]{:S(2)}) copy-start(f32[8,192,1]{2,1,0:T(8,128)S(1)} %copy.111) | copy-start | bytes 18436
  185.3 19.0 %copy-start.5 = (f32[8,192,1]{2,1,0:T(8,128)}, f32[8,192,1]{2,1,0:T(8,128)S(1)}, u32[]{:S(2)}) copy-start(f32[8,192,1]{2,1,0:T(8,128)S(1)} %copy.112) | copy-start | bytes 18436
  185.4 18.8 %collective-permute-start.15 = (f32[8,1,130]{2,0,1:T(8,128)S(1)}, f32[8,1,130]{2,0,1:T(8,128)S(1)}, u32[]{:S(2)}, u32[]{:S(2)}) collective-permute-start(f32[8,1,130]{2,0,1:T(8,128)S(1)} %copy.124), channel_id=1, source_target_pairs={{8,0},{16,8},{24,16},{9,1},{17,9},{25,17},{10,2},{18,10},{26,18},{... | collective-permute-start | bytes 12488 | tf_op jit(solution)/shard_map/ppermute | solution.py:19
  186.7 17.6 %collective-permute-start.14 = (f32[8,1,130]{2,0,1:T(8,128)S(1)}, f32[8,1,130]{2,0,1:T(8,128)S(1)}, u32[]{:S(2)}, u32[]{:S(2)}) collective-permute-start(f32[8,1,130]{2,0,1:T(8,128)S(1)} %copy.113), channel_id=1, source_target_pairs={{0,8},{8,16},{16,24},{1,9},{9,17},{17,25},{2,10},{10,18},{18,26},{... | collective-permute-start | bytes 12488 | tf_op jit(solution)/shard_map/ppermute | solution.py:17
  207.8 42.9 %copy-start.13 = (f32[8]{0:T(128)S(1)}, f32[8]{0:T(128)}, u32[]{:S(2)}) copy-start(f32[8]{0:T(128)} %copy-done.12) | copy-start | bytes 100
  207.8 42.9 %copy-start.14 = (f32[8]{0:T(128)S(1)}, f32[8]{0:T(128)}, u32[]{:S(2)}) copy-start(f32[8]{0:T(128)} %get-tuple-element.67) | copy-start | bytes 100
  207.8 42.9 %copy-start.2 = (f32[8,192,128]{2,1,0:T(8,128)S(1)}, f32[8,192,128]{2,1,0:T(8,128)}, u32[]{:S(2)}) copy-start(f32[8,192,128]{2,1,0:T(8,128)} %copy-done.1) | copy-start | bytes 2359300
  207.9 42.9 %copy-start.11 = (f32[8]{0:T(128)S(1)}, f32[8]{0:T(128)}, u32[]{:S(2)}) copy-start(f32[8]{0:T(128)} %copy-done.10) | copy-start | bytes 100
  207.9 42.9 %copy-start.16 = (f32[8]{0:T(128)S(1)}, f32[8]{0:T(128)}, u32[]{:S(2)}) copy-start(f32[8]{0:T(128)} %copy-done.15) | copy-start | bytes 100
where the time goes:
time: 255 us; the launch traced here: 254 us
  blocking collectives  166 us (65%)
  starting transfers between devices  30.2 us (12%)
  other arithmetic  29.4 us (12%)
  local copies, waits for them, and re-layouts  23 us (9%)
  waiting for transfers between devices  4.77 us (2%)
    psum x3, blocking collectives, paired_sums(): lax.psum((jnp.sum(residual * scaled, axis=(1, 2)), jnp.sum(scaled * image...  119 us
    all_gather x3, blocking collectives, operate(): whole_top = lax.all_gather(top_row, 'lon', axis=1, tiled=True)  33.6 us
    ppermute x8, starting transfers between devices, extended(): lax.ppermute(tail, axis, [(i, (i + 1) % count) for i in range(ends)])  15.2 us
    ppermute x8, starting transfers between devices, extended(): lax.ppermute(head, axis, [((i + 1) % count, i) for i in range(ends)])  15 us
    all_gather x1, blocking collectives, body(): whole_north = lax.all_gather(north_top, 'lon', axis=0, tiled=True)  13.4 us
    reduce_sum x3, other arithmetic, paired_sums(): jnp.sum(scaled * image, axis=(1, 2))  9.31 us
  transfers between devices with their start and end apart: 16, of which 4 were waited for; matrix products, arithmetic and copies ran while one was open for 7% of the time, Pallas kernels for 0%

commit v1 on v0

v1 whole, which is shorter than its diff:
```python
import functools

import jax
import jax.numpy as jnp
from jax import lax
from jax.experimental import pallas as pl
from jax.experimental.pallas import tpu as pltpu
from jax.sharding import PartitionSpec as P

ITERS = 3
MESH = pl.DeviceIdType.MESH
S_, SE_, SW_, N_, NE_, NW_ = range(6)


def kernel(
    lat_count, lon_count,
    rhs, center_hbm, coup_hbm, land_hbm, partner_hbm, sol_out, res_out,
    w, obuf, center, coup, land, partner,
    dmask, coef, rowtop, rowbot, colw, cole, rrow, rcol, rfold, red, rred_lon, rred_lat,
    load_sem, store_sem, row_ss, row_rs, col_ss, col_rs, fold_ss, fold_rs,
    rl_ss, rl_rs, rt_ss, rt_rs,
):
    f32 = jnp.float32
    members, rows, cols = rhs.shape
    groups = rows // 8
    halves = -(-rows // 120)
    half = rows // halves
    hgroups = half // 8
    la, lo = lax.axis_index("lat"), lax.axis_index("lon")
    lat_first, lat_last = la == 0, la == lat_count - 1
    north, south = lax.rem(la + 1, lat_count), lax.rem(la + lat_count - 1, lat_count)
    east, west = lax.rem(lo + 1, lon_count), lax.rem(lo + lon_count - 1, lon_count)
    lane = lax.broadcasted_iota(jnp.int32, (members, cols), 1)
    sub = lax.broadcasted_iota(jnp.int32, (8, cols), 0)

    loads = [
        pltpu.make_async_copy(center_hbm, center, load_sem.at[0]),
        pltpu.make_async_copy(coup_hbm, coup, load_sem.at[1]),
        pltpu.make_async_copy(land_hbm, land, load_sem.at[2]),
        pltpu.make_async_copy(partner_hbm, partner, load_sem.at[3]),
    ]
    for m in range(members):
        loads.append(pltpu.make_async_copy(
            rhs.at[m], w.at[0, pl.ds(0, rows), m], load_sem.at[4 + m]))
    for c in loads:
        c.start()

    barrier = pltpu.get_barrier_semaphore()
    partners = [(la, lax.rem(lo + d, lon_count)) for d in range(1, lon_count)]
    partners += [(lax.rem(la + d, lat_count), lo) for d in range(1, lat_count)]
    partners += [(north, east), (north, west), (south, east), (south, west)]
    for p in partners:
        pl.semaphore_signal(barrier, inc=1, device_id=p, device_id_type=MESH)

    for c in loads:
        c.wait()

    def roll(x, shift, axis=1):
        return pltpu.roll(x, shift, axis)

    for h in range(halves):
        def prep(gl, carry):
            pw, pe = carry
            g = h * hgroups + gl
            rs = pl.ds(pl.multiple_of(g * 8, 8), 8)
            dmask[rs, :] = land[rs, :].astype(f32) / center[rs, :]
            for r in range(8):
                j = g * 8 + r
                v = w[0, j] * dmask[pl.ds(j, 1), :]
                w[0, j] = v
                here = lane == gl * 8 + r
                pw = jnp.where(here, v[:, 0:1], pw)
                pe = jnp.where(here, v[:, cols - 1:cols], pe)
            return pw, pe
        zero = jnp.zeros((members, cols), f32)
        pw, pe = lax.fori_loop(0, hgroups, prep, (zero, zero))
        colw[0, h] = pw
        cole[0, h] = pe
    cw = jnp.zeros((8, cols), f32)
    ce = jnp.zeros((8, cols), f32)
    for g in range(groups):
        rs = pl.ds(g * 8, 8)
        ce = jnp.where(lane == g, coup[0, rs, cols - 1:cols], ce)
        ce = jnp.where(lane == groups + g, coup[2, rs, cols - 1:cols], ce)
        cw = jnp.where(lane == g, coup[3, rs, 0:1], cw)
    colw[0, halves] = cw
    cole[0, halves] = ce
    rowtop[0, 0] = w[0, rows - 1]
    rowbot[0, 0] = w[0, 0]
    top = [coup[c, pl.ds(rows - 1, 1), :] for c in range(4)]
    packed = jnp.zeros((8, cols), f32)
    for c in (1, 2, 3):
        packed = jnp.where(sub == c, top[c], packed)
    rowtop[0, 1] = packed

    pl.semaphore_wait(barrier, len(partners))

    def exchange(k):
        tops = 2 if k == 0 else 1
        depth = halves + 1 if k == 0 else halves
        cps = []

        def rcopy(src, slot, n, dev):
            cps.append(pltpu.make_async_remote_copy(
                src_ref=src.at[k, pl.ds(0, n)], dst_ref=rrow.at[k, slot, pl.ds(0, n)],
                send_sem=row_ss.at[k, slot], recv_sem=row_rs.at[k, slot],
                device_id=dev, device_id_type=MESH))
        rcopy(rowtop, SW_, tops, (north, east))
        rcopy(rowtop, SE_, tops, (north, west))
        rcopy(rowbot, NW_, 1, (south, east))
        rcopy(rowbot, NE_, 1, (south, west))
        rcopy(rowtop, S_, tops, (north, lo))
        rcopy(rowbot, N_, 1, (south, lo))
        for src, side, dev in ((colw, 0, west), (cole, 1, east)):
            cps.append(pltpu.make_async_remote_copy(
                src_ref=src.at[k, pl.ds(0, depth)], dst_ref=rcol.at[k, side, pl.ds(0, depth)],
                send_sem=col_ss.at[k, side], recv_sem=col_rs.at[k, side],
                device_id=(la, dev), device_id_type=MESH))
        folds = []
        for d in range(1, lon_count):
            folds.append(pltpu.make_async_remote_copy(
                src_ref=rowtop.at[k, pl.ds(0, tops)], dst_ref=rfold.at[k, d, pl.ds(0, tops)],
                send_sem=fold_ss.at[k, d], recv_sem=fold_rs.at[k, d],
                device_id=(la, lax.rem(lo + d, lon_count)), device_id_type=MESH))

        @pl.when(lat_last)
        def _():
            for c in folds:
                c.start()
        for c in cps:
            c.start()
        for c in cps:
            c.wait_recv()

        @pl.when(lat_last)
        def _():
            for c in folds:
                c.wait_recv()
        return cps, folds

    def folded(k, slot, own):
        mine = partner[pl.ds(lo, 1), :]
        out = jnp.zeros((8, cols), f32)
        for d in range(lon_count):
            data = own if d == 0 else rfold[k, d, slot]
            first = lax.rem(lo + lon_count - d, lon_count) * cols
            at = jnp.broadcast_to(mine - first, (8, cols))
            inside = jnp.logical_and(at >= 0, at < cols)
            at = jnp.clip(at, 0, cols - 1)
            got = jnp.take_along_axis(data, at, axis=1, mode="promise_in_bounds")
            out = jnp.where(inside, got, out)
        return out

    done = []
    lane8 = lax.broadcasted_iota(jnp.int32, (8, cols), 1)

    def coefficients():
        smsg, semsg, swmsg = rrow[0, S_, 1], rrow[0, SE_, 1], rrow[0, SW_, 1]
        keep = jnp.where(lat_first, 0.0, 1.0).astype(f32)
        under_n = roll(smsg, 7, 0) * keep
        under_ne = roll(roll(jnp.where(lane8 == cols - 1, swmsg, smsg), 1), 6, 0) * keep
        under_nw = roll(roll(jnp.where(lane8 == 0, semsg, smsg), cols - 1), 5, 0) * keep
        from_east, from_west = rcol[0, 0, halves], rcol[0, 1, halves]

        @pl.when(lat_last)
        def _():
            got = folded(0, 1, rowtop[0, 1])
            last = rows - 1
            coup[1, pl.ds(last, 1), :] = 0.5 * (coup[1, pl.ds(last, 1), :] + got[1:2, :])
            coup[2, pl.ds(last, 1), :] = jnp.zeros((1, cols), f32)
            coup[3, pl.ds(last, 1), :] = jnp.zeros((1, cols), f32)

        def step(g, carry):
            pn, pne, pnw = carry
            rs = pl.ds(pl.multiple_of(g * 8, 8), 8)
            d = dmask[rs, :]
            e, n, ne, nw = (coup[c, rs, :] for c in range(4))
            gw = roll(from_west, lax.rem(2 * cols - 1 - g, cols))
            gne = roll(from_west, lax.rem(2 * cols - 1 - groups - g, cols))
            gnw = roll(from_east, lax.rem(cols - g, cols))
            coef[0, rs, :] = e * d
            coef[1, rs, :] = roll(jnp.where(lane8 == cols - 1, gw, e), 1) * d
            coef[2, rs, :] = n * d
            ns = roll(n, 1, 0)
            coef[3, rs, :] = jnp.where(sub == 0, pn, ns) * d
            coef[4, rs, :] = ne * d
            nes = roll(roll(jnp.where(lane8 == cols - 1, gne, ne), 1), 1, 0)
            coef[5, rs, :] = jnp.where(sub == 0, pne, nes) * d
            coef[6, rs, :] = nw * d
            nws = roll(roll(jnp.where(lane8 == 0, gnw, nw), cols - 1), 1, 0)
            coef[7, rs, :] = jnp.where(sub == 0, pnw, nws) * d
            return ns, nes, nws
        lax.fori_loop(0, groups, step, (under_n, under_ne, under_nw))

    zero = jnp.zeros((members, cols), f32)
    moments = jnp.zeros((members, cols), f32)
    for k in range(ITERS):
        done.append(exchange(k))
        if k == 0:
            coefficients()
        w[k, rows] = rrow[k, N_, 0]

        @pl.when(lat_last)
        def _():
            w[k, rows] = folded(k, 0, w[k, rows - 1])

        def sides(v, ge, gw):
            ve = roll(jnp.where(lane == 0, ge, v), cols - 1)
            vw = roll(jnp.where(lane == cols - 1, gw, v), 1)
            return v, ve, vw

        prev = sides(rrow[k, S_, 0], rrow[k, SE_, 0], rrow[k, SW_, 0])
        gws, ges = [], []
        for h in range(halves):
            if h + 1 < halves:
                fe = roll(rcol[k, 0, h + 1], half)
                fw = roll(rcol[k, 1, h + 1], half)
            else:
                fe = roll(rrow[k, NE_, 0], half)
                fw = roll(rrow[k, NW_, 0], half + 1)
            ges.append(jnp.where(lane == half, fe, rcol[k, 0, h]))
            gws.append(jnp.where(lane == half, fw, rcol[k, 1, h]))
        cur = sides(w[k, 0], ges[0], roll(gws[0], cols - 1))
        acc0, acc1 = zero, zero
        for h in range(halves):
            ge_h, gw_h = ges[h], gws[h]

            def step(gl, carry):
                prev, cur, acc0, acc1, pw, pe = carry
                g = h * hgroups + gl
                back = lax.rem(cols - gl * 8, cols)
                ge = roll(ge_h, back)
                gw = roll(gw_h, back)
                for r in range(8):
                    j = g * 8 + r
                    nxt = sides(w[k, j + 1], roll(ge, cols - 1 - r), roll(gw, cols - 2 - r))
                    c = [coef[q, pl.ds(j, 1), :] for q in range(8)]
                    out = (c[0] * cur[1] + c[1] * cur[2]) + (c[2] * nxt[0] + c[3] * prev[0])
                    out = out + ((c[4] * nxt[1] + c[5] * prev[2]) + (c[6] * nxt[2] + c[7] * prev[1]))
                    w[k + 1, j] = out
                    t = center[pl.ds(j, 1), :] * cur[0]
                    acc0 = acc0 + t * cur[0]
                    acc1 = acc1 + t * out
                    if k + 1 < ITERS:
                        here = lane == gl * 8 + r
                        pw = jnp.where(here, out[:, 0:1], pw)
                        pe = jnp.where(here, out[:, cols - 1:cols], pe)
                    prev, cur = cur, nxt
                return prev, cur, acc0, acc1, pw, pe
            prev, cur, acc0, acc1, pw, pe = lax.fori_loop(
                0, hgroups, step, (prev, cur, acc0, acc1, zero, zero))
            if k + 1 < ITERS:
                colw[k + 1, h] = pw
                cole[k + 1, h] = pe
        if k + 1 < ITERS:
            rowtop[k + 1, 0] = w[k + 1, rows - 1]
            rowbot[k + 1, 0] = w[k + 1, 0]
        moments = jnp.where(lane == 2 * k, jnp.sum(acc0, axis=1, keepdims=True), moments)
        moments = jnp.where(lane == 2 * k + 1, jnp.sum(acc1, axis=1, keepdims=True), moments)

    def reduce(slot, value, recv, ss, rs, count, dev):
        red[slot] = value
        cps = [
            pltpu.make_async_remote_copy(
                src_ref=red.at[slot], dst_ref=recv.at[d], send_sem=ss.at[d],
                recv_sem=rs.at[d], device_id=dev(d), device_id_type=MESH)
            for d in range(1, count)
        ]
        for c in cps:
            c.start()
        for c in cps:
            c.wait_recv()
        for d in range(1, count):
            value = value + recv[d]
        return value, cps

    moments, c1 = reduce(0, moments, rred_lon, rl_ss, rl_rs, lon_count,
                         lambda d: (la, lax.rem(lo + d, lon_count)))
    moments, c2 = reduce(1, moments, rred_lat, rt_ss, rt_rs, lat_count,
                         lambda d: (lax.rem(la + d, lat_count), lo))

    m0, m1, m2, m3, m4, m5 = (
        jnp.broadcast_to(moments[:, i:i + 1], (members, cols)) for i in range(6))
    a0 = m1 / m0
    h1 = m2 - a0 * m1
    a1 = (m3 - 2.0 * a0 * m2 + a0 * a0 * m1) / h1
    b1 = h1 / m0
    p1 = -(a0 + a1)
    p0 = a0 * a1 - b1
    h2 = m4 + p1 * m3 + p0 * m2
    a2 = (m5 + p1 * m4 + p0 * m3) / h2 + p1
    b2 = h2 / h1
    t2 = p1 - a2
    t1 = p0 - a2 * p1 - b2
    t0 = b2 * a0 - a2 * p0
    q3 = 1.0 / (1.0 + t2 + t1 + t0)
    q2, q1, q0 = t2 * q3, t1 * q3, t0 * q3
    s2, s1, s0 = q3, q2 + q3, q1 + q2 + q3

    chunk = 4
    stores = []
    for c in range(chunk):
        size = groups // chunk

        def final(g, carry):
            for r in range(8):
                j = (c * size + g) * 8 + r
                v0, v1, v2, v3 = (w[i, j] for i in range(4))
                obuf[0, j] = s0 * v0 + s1 * v1 + s2 * v2
                obuf[1, j] = center[pl.ds(j, 1), :] * (q0 * v0 + q1 * v1 + q2 * v2 + q3 * v3)
            return carry
        lax.fori_loop(0, size, final, 0)
        rs = pl.ds(c * size * 8, size * 8)
        for o, dst in ((0, sol_out), (1, res_out)):
            for m in range(members):
                cp = pltpu.make_async_copy(
                    obuf.at[o, rs, m], dst.at[m, rs], store_sem.at[c, o, m])
                cp.start()
                stores.append(cp)
    for cps, folds in done:
        for cp in cps:
            cp.wait_send()

        @pl.when(lat_last)
        def _():
            for cp in folds:
                cp.wait_send()
    for cp in c1 + c2:
        cp.wait_send()
    for cp in stores:
        cp.wait()


def body(lat_count, lon_count, right_side, center, couplings, land_sea, fold_partner):
    members, rows, cols = right_side.shape
    f32 = jnp.float32
    halves = -(-rows // 120)
    hbm = pl.BlockSpec(memory_space=pl.ANY)
    dma = pltpu.SemaphoreType.DMA
    shape = jax.ShapeDtypeStruct(right_side.shape, f32)
    return pl.pallas_call(
        functools.partial(kernel, lat_count, lon_count),
        out_shape=(shape, shape),
        in_specs=[hbm] * 5,
        out_specs=(hbm, hbm),
        scratch_shapes=[
            pltpu.VMEM((ITERS + 1, rows + 1, members, cols), f32),
            pltpu.VMEM((2, rows, members, cols), f32),
            pltpu.VMEM((rows, cols), f32),
            pltpu.VMEM((4, rows, cols), f32),
            pltpu.VMEM((rows, cols), jnp.int32),
            pltpu.VMEM((lon_count, cols), jnp.int32),
            pltpu.VMEM((rows, cols), f32),
            pltpu.VMEM((8, rows, cols), f32),
            pltpu.VMEM((ITERS, 2, 8, cols), f32),
            pltpu.VMEM((ITERS, 1, 8, cols), f32),
            pltpu.VMEM((ITERS, halves + 1, 8, cols), f32),
            pltpu.VMEM((ITERS, halves + 1, 8, cols), f32),
            pltpu.VMEM((ITERS, 6, 2, 8, cols), f32),
            pltpu.VMEM((ITERS, 2, halves + 1, 8, cols), f32),
            pltpu.VMEM((ITERS, lon_count, 2, 8, cols), f32),
            pltpu.VMEM((2, 8, cols), f32),
            pltpu.VMEM((lon_count, 8, cols), f32),
            pltpu.VMEM((lat_count, 8, cols), f32),
            dma((4 + members,)),
            dma((4, 2, members)),
            dma((ITERS, 6)), dma((ITERS, 6)),
            dma((ITERS, 2)), dma((ITERS, 2)),
            dma((ITERS, lon_count)), dma((ITERS, lon_count)),
            dma((lon_count,)), dma((lon_count,)),
            dma((lat_count,)), dma((lat_count,)),
        ],
        compiler_params=pltpu.CompilerParams(
            collective_id=0, has_side_effects=True, vmem_limit_bytes=40 * 1024 * 1024),
    )(right_side, center, couplings, land_sea, fold_partner.reshape(lon_count, cols))


def solution(mesh):
    return jax.shard_map(
        functools.partial(body, mesh.shape["lat"], mesh.shape["lon"]),
        mesh=mesh,
        in_specs=(
            P(None, "lat", "lon"),
            P("lat", "lon"),
            P(None, "lat", "lon"),
            P("lat", "lon"),
            P(),
        ),
        out_specs=(P(None, "lat", "lon"), P(None, "lat", "lon")),
        check_vma=False,
    )
```

time: 255 us -> 61.6 us (0.24)
  blocking collectives: 166 us -> 0 us
  Pallas kernels: 0 us -> 54.3 us
  starting transfers between devices: 30.2 us -> 0 us
  other arithmetic: 29.4 us -> 0 us
  local copies, waits for them, and re-layouts: 23 us -> 6.35 us
  waiting for transfers between devices: 4.77 us -> 0 us
    psum x3 -> x0, blocking collectives: 119 us -> none  [paired_sums(): lax.psum((jnp.sum(residual * scaled, axis=(1, 2)), jnp.sum(scaled * image...]
    pallas_call x0 -> x1, Pallas kernels: none -> 54.3 us  [body(): pl.pallas_call(functools.partial(kernel, lat_count, lon_count), out_shape...]
    all_gather x4 -> x0, blocking collectives: 47.1 us -> none  [the longest x3 33.6 us: operate(): whole_top = lax.all_gather(top_row, 'lon', axis=1, tiled=True)]
    ppermute x16 -> x0, starting transfers between devices: 30.2 us -> none  [the longest x8 15.2 us: extended(): lax.ppermute(tail, axis, [(i, (i + 1) % count) for i in range(ends)])]
    reduce_sum x3 -> x0, other arithmetic: 9.31 us -> none  [paired_sums(): jnp.sum(scaled * image, axis=(1, 2))]
    slice x16 -> x0, local copies, waits for them, and re-layouts: 6.58 us -> none  [the longest x9 3.67 us: extended(): lax.slice_in_dim(cells, cells.shape[dim] - width, cells.shape[dim], axis=...]
    unnamed x44 -> x12, local copies, waits for them, and re-layouts: 0.11 us -> 6.35 us
    div x6 -> x0, other arithmetic: 5.51 us -> none  [the longest x3 4.9 us: body(): scaled = residual / center]
  transfers between devices with their start and end apart: 16 -> 0, of which waited for: 4 -> 0; matrix products, arithmetic and copies ran while one was open for 7% -> 0% of each run, Pallas kernels for 0% -> 0%
where the time goes in v1:
time: 61.6 us; the launch traced here: 61.3 us
  Pallas kernels  54.3 us (88%)
  local copies, waits for them, and re-layouts  6.35 us (10%)
  between operations  0.65 us (1%)
    pallas_call x1, Pallas kernels, body(): pl.pallas_call(functools.partial(kernel, lat_count, lon_count), out_shape...  54.3 us
    unnamed x12, local copies, waits for them, and re-layouts  6.35 us

profile of v1, /device:TPU:0, one launch (start us, length us, event | category | flops | bytes accessed | tf_op | source)
XLA Modules:
  0.0 61.3 jit_solution(10401661890124015602)
XLA Ops:
  0.6 0.0 copy-start
  0.6 1.1 %copy-done = f32[8,192,128]{2,1,0:T(8,128)S(1)} copy-done((f32[8,192,128]{2,1,0:T(8,128)S(1)}, f32[8,192,128]{2,1,0:T(8,128)}, u32[]{:S(2)}) %copy-start) | copy-done | bytes 786456
  1.8 0.0 copy-start.1
  1.8 1.0 %copy-done.1 = f32[4,192,128]{2,1,0:T(8,128)S(1)} copy-done((f32[4,192,128]{2,1,0:T(8,128)S(1)}, f32[4,192,128]{2,1,0:T(8,128)}, u32[]{:S(2)}) %copy-start.1) | copy-done | bytes 393240
  2.8 0.0 copy-start.2
  2.8 0.9 %copy-done.2 = f32[192,128]{1,0:T(8,128)S(1)} copy-done((f32[192,128]{1,0:T(8,128)S(1)}, f32[192,128]{1,0:T(8,128)}, u32[]{:S(2)}) %copy-start.2) | copy-done | bytes 98328
  3.7 0.0 copy-start.3
  3.7 0.9 %copy-done.3 = s32[192,128]{1,0:T(8,128)S(1)} copy-done((s32[192,128]{1,0:T(8,128)S(1)}, s32[192,128]{1,0:T(8,128)}, u32[]{:S(2)}) %copy-start.3) | copy-done | bytes 98328
  4.5 0.0 copy-start.4
  4.5 0.7 %copy-done.4 = s32[1024]{0:T(1024)S(1)} copy-done((s32[1024]{0:T(1024)S(1)}, s32[1024]{0:T(1024)}, u32[]{:S(2)}) %copy-start.4) | copy-done | bytes 4120
  5.2 54.3 %shard_map.68 = (f32[8,192,128]{2,1,0:T(8,128)S(1)}, f32[8,192,128]{2,1,0:T(8,128)S(1)}) custom-call(f32[8,192,128]{2,1,0:T(8,128)S(1)} %copy-done, f32[192,128]{1,0:T(8,128)S(1)} %copy-done.2, f32[4,192,128]{2,1,0:T(8,128)S(1)} %copy-done.1, s32[192,128]{1,0:T(8,128)S(1)} %copy-done.3, s32[8,128]{1,0:T(8,128)S(1)} %bitcast.1), custom_call_target="tpu_custom_call" | custom-call | tf_op jit(solution)/shard_map/pallas_call | solution.py:341
  59.5 0.9 %copy.9 = f32[8,192,128]{2,1,0:T(8,128)} copy(f32[8,192,128]{2,1,0:T(8,128)S(1)} %get-tuple-element.4) | data formatting | bytes 1572864
  60.4 0.9 %copy.10 = f32[8,192,128]{2,1,0:T(8,128)} copy(f32[8,192,128]{2,1,0:T(8,128)S(1)} %get-tuple-element.5) | data formatting | bytes 1572864
Async XLA Ops:
  0.6 1.1 %copy-start = (f32[8,192,128]{2,1,0:T(8,128)S(1)}, f32[8,192,128]{2,1,0:T(8,128)}, u32[]{:S(2)}) copy-start(f32[8,192,128]{2,1,0:T(8,128)} %rhs.1) | copy-start | bytes 2359300
  1.8 1.0 %copy-start.1 = (f32[4,192,128]{2,1,0:T(8,128)S(1)}, f32[4,192,128]{2,1,0:T(8,128)}, u32[]{:S(2)}) copy-start(f32[4,192,128]{2,1,0:T(8,128)} %coup_hbm.1) | copy-start | bytes 1179652
  2.8 0.9 %copy-start.2 = (f32[192,128]{1,0:T(8,128)S(1)}, f32[192,128]{1,0:T(8,128)}, u32[]{:S(2)}) copy-start(f32[192,128]{1,0:T(8,128)} %center_hbm.1) | copy-start | bytes 294916
  3.7 0.9 %copy-start.3 = (s32[192,128]{1,0:T(8,128)S(1)}, s32[192,128]{1,0:T(8,128)}, u32[]{:S(2)}) copy-start(s32[192,128]{1,0:T(8,128)} %land_hbm.1) | copy-start | bytes 294916
  4.5 0.7 %copy-start.4 = (s32[1024]{0:T(1024)S(1)}, s32[1024]{0:T(1024)}, u32[]{:S(2)}) copy-start(s32[1024]{0:T(1024)} %param.9) | copy-start | bytes 12292

commit v2 on v1

--- a/solution.py
+++ b/solution.py
@@ -25,7 +25,8 @@
     groups = rows // 8
     halves = -(-rows // 120)
     half = rows // halves
-    hgroups = half // 8
+    step_rows = 16 if half % 16 == 0 else 8
+    steps = half // step_rows
     la, lo = lax.axis_index("lat"), lax.axis_index("lon")
     lat_first, lat_last = la == 0, la == lat_count - 1
     north, south = lax.rem(la + 1, lat_count), lax.rem(la + lat_count - 1, lat_count)
@@ -58,31 +59,37 @@
     def roll(x, shift, axis=1):
         return pltpu.roll(x, shift, axis)
 
+    def packed_step(pw, pe, values):
+        pw, pe = roll(pw, cols - step_rows), roll(pe, cols - step_rows)
+        for r, v in enumerate(values):
+            at = cols - step_rows + r
+            pw = jnp.where(lane == at, roll(v, at), pw)
+            pe = jnp.where(lane == at, roll(v, (at + 1) % cols), pe)
+        return pw, pe
+
     for h in range(halves):
         def prep(gl, carry):
             pw, pe = carry
-            g = h * hgroups + gl
-            rs = pl.ds(pl.multiple_of(g * 8, 8), 8)
+            j0 = pl.multiple_of((h * steps + gl) * step_rows, 8)
+            rs = pl.ds(j0, step_rows)
             dmask[rs, :] = land[rs, :].astype(f32) / center[rs, :]
-            for r in range(8):
-                j = g * 8 + r
-                v = w[0, j] * dmask[pl.ds(j, 1), :]
-                w[0, j] = v
-                here = lane == gl * 8 + r
-                pw = jnp.where(here, v[:, 0:1], pw)
-                pe = jnp.where(here, v[:, cols - 1:cols], pe)
-            return pw, pe
+            values = []
+            for r in range(step_rows):
+                v = w[0, j0 + r] * dmask[pl.ds(j0 + r, 1), :]
+                w[0, j0 + r] = v
+                values.append(v)
+            return packed_step(pw, pe, values)
         zero = jnp.zeros((members, cols), f32)
-        pw, pe = lax.fori_loop(0, hgroups, prep, (zero, zero))
-        colw[0, h] = pw
-        cole[0, h] = pe
+        pw, pe = lax.fori_loop(0, steps, prep, (zero, zero))
+        colw[0, h] = roll(pw, half)
+        cole[0, h] = roll(pe, half)
     cw = jnp.zeros((8, cols), f32)
     ce = jnp.zeros((8, cols), f32)
     for g in range(groups):
         rs = pl.ds(g * 8, 8)
-        ce = jnp.where(lane == g, coup[0, rs, cols - 1:cols], ce)
-        ce = jnp.where(lane == groups + g, coup[2, rs, cols - 1:cols], ce)
-        cw = jnp.where(lane == g, coup[3, rs, 0:1], cw)
+        ce = jnp.where(lane == g, roll(coup[0, rs, :], g + 1), ce)
+        ce = jnp.where(lane == groups + g, roll(coup[2, rs, :], groups + g + 1), ce)
+        cw = jnp.where(lane == g, roll(coup[3, rs, :], g) if g else coup[3, rs, :], cw)
     colw[0, halves] = cw
     cole[0, halves] = ce
     rowtop[0, 0] = w[0, rows - 1]
@@ -95,7 +102,7 @@
 
     pl.semaphore_wait(barrier, len(partners))
 
-    def exchange(k):
+    def exchange(k, between):
         tops = 2 if k == 0 else 1
         depth = halves + 1 if k == 0 else halves
         cps = []
@@ -129,6 +136,7 @@
                 c.start()
         for c in cps:
             c.start()
+        between()
         for c in cps:
             c.wait_recv()
 
@@ -193,9 +201,15 @@
         lax.fori_loop(0, groups, step, (under_n, under_ne, under_nw))
 
     zero = jnp.zeros((members, cols), f32)
-    moments = jnp.zeros((members, cols), f32)
+    sums = []
+
+    def add_sums():
+        for acc in accs:
+            sums.append(jnp.sum(acc, axis=1, keepdims=True))
+
+    accs = []
     for k in range(ITERS):
-        done.append(exchange(k))
+        done.append(exchange(k, add_sums))
         if k == 0:
             coefficients()
         w[k, rows] = rrow[k, N_, 0]
@@ -226,13 +240,11 @@
             ge_h, gw_h = ges[h], gws[h]
 
             def step(gl, carry):
-                prev, cur, acc0, acc1, pw, pe = carry
-                g = h * hgroups + gl
-                back = lax.rem(cols - gl * 8, cols)
-                ge = roll(ge_h, back)
-                gw = roll(gw_h, back)
-                for r in range(8):
-                    j = g * 8 + r
+                prev, cur, acc0, acc1, pw, pe, ge, gw = carry
+                j0 = pl.multiple_of((h * steps + gl) * step_rows, 8)
+                values = []
+                for r in range(step_rows):
+                    j = j0 + r
                     nxt = sides(w[k, j + 1], roll(ge, cols - 1 - r), roll(gw, cols - 2 - r))
                     c = [coef[q, pl.ds(j, 1), :] for q in range(8)]
                     out = (c[0] * cur[1] + c[1] * cur[2]) + (c[2] * nxt[0] + c[3] * prev[0])
@@ -241,22 +253,25 @@
                     t = center[pl.ds(j, 1), :] * cur[0]
                     acc0 = acc0 + t * cur[0]
                     acc1 = acc1 + t * out
-                    if k + 1 < ITERS:
-                        here = lane == gl * 8 + r
-                        pw = jnp.where(here, out[:, 0:1], pw)
-                        pe = jnp.where(here, out[:, cols - 1:cols], pe)
+                    values.append(out)
                     prev, cur = cur, nxt
-                return prev, cur, acc0, acc1, pw, pe
-            prev, cur, acc0, acc1, pw, pe = lax.fori_loop(
-                0, hgroups, step, (prev, cur, acc0, acc1, zero, zero))
+                if k + 1 < ITERS:
+                    pw, pe = packed_step(pw, pe, values)
+                ge, gw = roll(ge, cols - step_rows), roll(gw, cols - step_rows)
+                return prev, cur, acc0, acc1, pw, pe, ge, gw
+            prev, cur, acc0, acc1, pw, pe, _, _ = lax.fori_loop(
+                0, steps, step, (prev, cur, acc0, acc1, zero, zero, ge_h, gw_h))
             if k + 1 < ITERS:
-                colw[k + 1, h] = pw
-                cole[k + 1, h] = pe
+                colw[k + 1, h] = roll(pw, half)
+                cole[k + 1, h] = roll(pe, half)
         if k + 1 < ITERS:
             rowtop[k + 1, 0] = w[k + 1, rows - 1]
             rowbot[k + 1, 0] = w[k + 1, 0]
-        moments = jnp.where(lane == 2 * k, jnp.sum(acc0, axis=1, keepdims=True), moments)
-        moments = jnp.where(lane == 2 * k + 1, jnp.sum(acc1, axis=1, keepdims=True), moments)
+        accs[:] = [acc0, acc1]
+    add_sums()
+    moments = zero
+    for i, total in enumerate(sums):
+        moments = jnp.where(lane == i, total, moments)
 
     def reduce(slot, value, recv, ss, rs, count, dev):
         red[slot] = value
@@ -371,7 +386,7 @@
             dma((lat_count,)), dma((lat_count,)),
         ],
         compiler_params=pltpu.CompilerParams(
-            collective_id=0, has_side_effects=True, vmem_limit_bytes=40 * 1024 * 1024),
+            collective_id=0, has_side_effects=True, vmem_limit_bytes=67043328),
     )(right_side, center, couplings, land_sea, fold_partner.reshape(lon_count, cols))
 
 

time: 61.6 us -> 45 us (0.73)
  Pallas kernels: 54.3 us -> 41.1 us
  local copies, waits for them, and re-layouts: 6.35 us -> 3.03 us
    pallas_call x1, Pallas kernels: 54.3 us -> 41.1 us  [body(): pl.pallas_call(functools.partial(kernel, lat_count, lon_count), out_shape...]
    unnamed x12 -> x4, local copies, waits for them, and re-layouts: 6.35 us -> 3.03 us
where the time goes in v2:
time: 45 us; the launch traced here: 44.8 us
  Pallas kernels  41.1 us (91%)
  local copies, waits for them, and re-layouts  3.03 us (7%)
  between operations  0.65 us (1%)
    pallas_call x1, Pallas kernels, body(): pl.pallas_call(functools.partial(kernel, lat_count, lon_count), out_shape...  41.1 us
    unnamed x4, local copies, waits for them, and re-layouts  3.03 us

profile of v2, /device:TPU:0, one launch (start us, length us, event | category | flops | bytes accessed | tf_op | source)
XLA Modules:
  0.0 44.8 jit_solution(1847061810779937790)
XLA Ops:
  0.6 41.1 %shard_map.68 = (f32[8,192,128]{2,1,0:T(8,128)}, f32[8,192,128]{2,1,0:T(8,128)}) custom-call(f32[8,192,128]{2,1,0:T(8,128)} %rhs.1, f32[192,128]{1,0:T(8,128)} %center_hbm.1, f32[4,192,128]{2,1,0:T(8,128)} %coup_hbm.1, s32[192,128]{1,0:T(8,128)} %land_hbm.1, s32[8,128]{1,0:T(8,128)} %bitcast.1), custom_call_target="tpu_custom_call" | custom-call | tf_op jit(solution)/shard_map/pallas_call | solution.py:356
  41.8 0.0 copy-start
  41.8 2.1 %copy.9 = f32[8,192,128]{2,1,0:T(8,128)} copy(f32[8,192,128]{2,1,0:T(8,128)} %get-tuple-element.4) | data formatting | bytes 1572864
  43.9 0.0 copy-done
  43.9 0.9 %copy.10 = f32[8,192,128]{2,1,0:T(8,128)} copy(f32[8,192,128]{2,1,0:T(8,128)S(1)} %copy-done) | data formatting | bytes 1572864
Async XLA Ops:
  41.8 2.2 %copy-start = (f32[8,192,128]{2,1,0:T(8,128)S(1)}, f32[8,192,128]{2,1,0:T(8,128)}, u32[]{:S(2)}) copy-start(f32[8,192,128]{2,1,0:T(8,128)} %get-tuple-element.5) | copy-start | bytes 2359300

commit v3 on v2

--- a/solution.py
+++ b/solution.py
@@ -25,7 +25,7 @@
     groups = rows // 8
     halves = -(-rows // 120)
     half = rows // halves
-    step_rows = 16 if half % 16 == 0 else 8
+    step_rows = 24 if half % 24 == 0 else 8
     steps = half // step_rows
     la, lo = lax.axis_index("lat"), lax.axis_index("lon")
     lat_first, lat_last = la == 0, la == lat_count - 1
@@ -198,7 +198,7 @@
             nws = roll(roll(jnp.where(lane8 == 0, gnw, nw), cols - 1), 1, 0)
             coef[7, rs, :] = jnp.where(sub == 0, pnw, nws) * d
             return ns, nes, nws
-        lax.fori_loop(0, groups, step, (under_n, under_ne, under_nw))
+        lax.fori_loop(0, groups, step, (under_n, under_ne, under_nw), unroll=12)
 
     zero = jnp.zeros((members, cols), f32)
     sums = []

time: 45 us -> 39.8 us (0.88)
  Pallas kernels: 41.1 us -> 36 us
    pallas_call x1, Pallas kernels: 41.1 us -> 36 us  [body(): pl.pallas_call(functools.partial(kernel, lat_count, lon_count), out_shape...]
where the time goes in v3:
time: 39.8 us; the launch traced here: 39.6 us
  Pallas kernels  36 us (90%)
  local copies, waits for them, and re-layouts  3.03 us (8%)
  between operations  0.65 us (2%)
    pallas_call x1, Pallas kernels, body(): pl.pallas_call(functools.partial(kernel, lat_count, lon_count), out_shape...  36 us
    unnamed x4, local copies, waits for them, and re-layouts  3.03 us

profile of v3, /device:TPU:0, one launch (start us, length us, event | category | flops | bytes accessed | tf_op | source)
XLA Modules:
  0.0 39.6 jit_solution(8257925044675569014)
XLA Ops:
  0.6 36.0 %shard_map.68 = (f32[8,192,128]{2,1,0:T(8,128)}, f32[8,192,128]{2,1,0:T(8,128)}) custom-call(f32[8,192,128]{2,1,0:T(8,128)} %rhs.1, f32[192,128]{1,0:T(8,128)} %center_hbm.1, f32[4,192,128]{2,1,0:T(8,128)} %coup_hbm.1, s32[192,128]{1,0:T(8,128)} %land_hbm.1, s32[8,128]{1,0:T(8,128)} %bitcast.1), custom_call_target="tpu_custom_call" | custom-call | tf_op jit(solution)/shard_map/pallas_call | solution.py:356
  36.6 0.0 copy-start
  36.6 2.1 %copy.9 = f32[8,192,128]{2,1,0:T(8,128)} copy(f32[8,192,128]{2,1,0:T(8,128)} %get-tuple-element.4) | data formatting | bytes 1572864
  38.8 0.0 copy-done
  38.8 0.9 %copy.10 = f32[8,192,128]{2,1,0:T(8,128)} copy(f32[8,192,128]{2,1,0:T(8,128)S(1)} %copy-done) | data formatting | bytes 1572864
Async XLA Ops:
  36.6 2.2 %copy-start = (f32[8,192,128]{2,1,0:T(8,128)S(1)}, f32[8,192,128]{2,1,0:T(8,128)}, u32[]{:S(2)}) copy-start(f32[8,192,128]{2,1,0:T(8,128)} %get-tuple-element.5) | copy-start | bytes 2359300
